TPU v7x, 32 devices: a whole 2x2x4 slice. The times are simulated.
32 devices in a mesh: clip: 2 (over y), ha: 8 (over z, x), ta: 2 (over core).
Axes of the slice: x: 2, y: 2, z: 4, core: 2. Of those that a mesh axis runs over, the one named last changes fastest.
Arguments:
- latent_tokens: bfloat16 [16, 512, 64], P('clip', ('ha', 'ta')), parts along dimension 0, may hold values from -8 to 8
- w_in: bfloat16 [3, 3, 3, 16, 384], replicated, may hold values from -0.3125 to 0.3125
- b_in: float32 [384], replicated, may hold values from -3 to 3
- gn_gain: float32 [384], replicated, may hold values from 0.1 to 1.9
- gn_shift: float32 [384], replicated, may hold values from -3 to 3
- w_mid: bfloat16 [3, 3, 3, 384, 384], replicated, may hold values from -0.109375 to 0.109375
- b_mid: float32 [384], replicated, may hold values from -3 to 3
Outputs:
- decoded: bfloat16 [16, 16, 128, 384], P(('clip', 'ta'), 'ha'), parts along dimension 0
There are 2 independent parts, one for each index of `clip`. A program takes and returns all parts, laid end to end along the dimension named above; an argument that names none is the same for every part. Nothing has to cross between parts.
All inputs are finite; a program needn't handle non-finite values.
Results may differ from a plain program's by a relative error of at most 0.0054.
Values may be sent and summed in bfloat16 or wider, within the bound.
A program may use at most 64 MiB of HBM per device.

v0:
```python
import jax
import jax.numpy as jnp
from jax import lax
from jax.sharding import PartitionSpec as P

GROUPS = 32
H_DEV = 2
W = 128
eps = 1e-06


def passed_along(value, axis, by):
    devices = lax.axis_size(axis)
    pairs = [(i, i + by) for i in range(devices) if 0 <= i + by < devices]
    return lax.ppermute(value, axis, pairs)


def extended_2(value, sides, width):
    for axis, dim in sides:
        devices, length = (lax.axis_size(axis), value.shape[dim])
        up = [(i, (i + 1) % devices) for i in range(devices - 1)]
        down = [(j, i) for i, j in up]
        last = lax.slice_in_dim(value, length - width, length, axis=dim)
        first = lax.slice_in_dim(value, 0, width, axis=dim)
        before = lax.ppermute(last, axis, up)
        after = lax.ppermute(first, axis, down)
        value = jnp.concatenate([before, value, after], axis=dim)
    return value


def unpatch(tokens, rows, cols):
    frames = tokens.shape[0]
    latent_ch = tokens.shape[2] // 4
    blocks = tokens.reshape(frames, rows // 2, cols // 2, 2, 2, latent_ch)
    return blocks.transpose(0, 1, 3, 2, 4, 5).reshape(frames, rows, cols, latent_ch)


def pad_cols(field):
    return jnp.pad(field, ((0, 0), (0, 0), (1, 1), (0, 0)))


def input_conv(padded, w_in, b_in, frames, rows, cols):
    pieces = [
        padded[frame_tap : frame_tap + frames, row_tap : row_tap + rows, col_tap : col_tap + cols]
        for frame_tap in range(3)
        for row_tap in range(3)
        for col_tap in range(3)
    ]
    stacked = jnp.concatenate(pieces, axis=-1).reshape(frames * rows * cols, -1)
    result = jnp.dot(
        stacked, w_in.reshape(stacked.shape[1], -1), preferred_element_type=jnp.float32
    )
    return (result + b_in).reshape(frames, rows, cols, -1)


def middle_conv(padded, w_mid, frames, rows, cols):
    channels = padded.shape[-1]
    total = jnp.zeros((frames * rows * cols, w_mid.shape[-1]), jnp.float32)
    for frame_tap in range(3):
        for row_tap in range(3):
            slab = jnp.concatenate(
                [
                    padded[
                        frame_tap : frame_tap + frames,
                        row_tap : row_tap + rows,
                        col_tap : col_tap + cols,
                    ]
                    for col_tap in range(3)
                ],
                axis=-1,
            ).reshape(frames * rows * cols, 3 * channels)
            total = total + jnp.dot(
                slab,
                w_mid[frame_tap, row_tap].reshape(3 * channels, -1),
                preferred_element_type=jnp.float32,
            )
    return total.reshape(frames, rows, cols, -1)


def group_totals(field):
    grouped = field.reshape(-1, GROUPS, field.shape[-1] // GROUPS)
    return jnp.sum(grouped, axis=(0, 2))


def normalize(hidden, mean, var, gn_gain, gn_shift):
    members = hidden.shape[-1] // GROUPS
    mean_chan = jnp.repeat(mean, members)
    scale_chan = jnp.repeat(lax.rsqrt(var + eps), members)
    scaled = (hidden.astype(jnp.float32) - mean_chan) * scale_chan * gn_gain + gn_shift
    return jax.nn.silu(scaled).astype(jnp.bfloat16)


def body(latent_tokens, w_in, b_in, gn_gain, gn_shift, w_mid, b_mid):
    rows = H_DEV
    cols = W
    moved = lax.all_to_all(latent_tokens, "ta", split_axis=0, concat_axis=1, tiled=True)
    latent = unpatch(moved, rows, cols)
    frames = latent.shape[0]
    earlier = passed_along(latent, "ta", 1)
    extended = jnp.concatenate([earlier, latent], axis=0)
    framed = extended_2(extended, (("ha", 1),), 2)
    wide_hidden = input_conv(pad_cols(framed), w_in, b_in, frames + 2, rows + 2, cols).astype(
        jnp.bfloat16
    )
    hidden = wide_hidden[2:, 1 : rows + 1]
    values = lax.optimization_barrier(hidden).astype(jnp.float32)
    members = values.shape[-1] // GROUPS
    count = float(lax.axis_size("ha") * lax.axis_size("ta") * frames * rows * cols * members)
    mean = lax.psum(group_totals(values), ("ha", "ta")) / count
    centered = values - jnp.repeat(mean, members)
    var = lax.psum(group_totals(centered * centered), ("ha", "ta")) / count
    active = normalize(wide_hidden, mean, var, gn_gain, gn_shift)
    frame_pos = lax.axis_index("ta") * frames + jnp.arange(frames + 2, dtype=jnp.int32) - 2
    row_pos = lax.axis_index("ha") * rows + jnp.arange(rows + 2, dtype=jnp.int32) - 1
    inside = (
        (frame_pos >= 0)[:, None]
        & (row_pos >= 0)[None, :]
        & (row_pos < rows * lax.axis_size("ha"))[None, :]
    )
    padded = jnp.where(inside[:, :, None, None], active, jnp.zeros_like(active))
    branch = middle_conv(pad_cols(padded), w_mid, frames, rows, cols)
    return (values + branch + b_mid).astype(jnp.bfloat16)


def solution(mesh):
    placed = (P("clip", ("ha", "ta"), None), P(), P(), P(), P(), P(), P())
    return jax.shard_map(
        body,
        mesh=mesh,
        in_specs=placed,
        out_specs=P(("clip", "ta"), "ha", None, None),
        check_vma=False,
    )
```

profile of v0, /device:TPU:0, one launch (start us, length us, event | category | flops | bytes accessed | tf_op | source)
XLA Modules:
  0.0 131.4 jit_solution(58256040233946923)
XLA Ops:
  1.0 3.7 %all_to_all.15 = bf16[2,2,4096]{2,1,0:T(2,128)(2,1)S(1)} all-to-all(bf16[2,2,4096]{2,1,0:T(2,128)(2,1)S(1)} %reshape.124), channel_id=1, replica_groups=mesh['clip'=2,'ha'=8,'ta'=2] {'ta'}, dimensions={0} | all-to-all | bytes 65536 | tf_op jit(solution)/shard_map/all_to_all | solution.py:96
  5.3 2.1 %collective-permute-start = (bf16[4,2,128,16]{3,2,1,0:T(8,128)(2,1)S(1)}, bf16[4,2,128,16]{3,2,1,0:T(8,128)(2,1)S(1)}, u32[]{:S(2)}, u32[]{:S(2)}) collective-permute-start(bf16[4,2,128,16]{3,2,1,0:T(8,128)(2,1)S(1)} %bitcast.63), channel_id=1, source_target_pairs={{0,1},{2,3},{4,5},{6,7},{8,9},{10,11},{12,13},{14,15},{16,17},{18,... | collective-permute-start | bytes 98312 | tf_op jit(solution)/shard_map/ppermute | solution.py:15
  7.4 5.7 %fusion.25 = (bf16[1,1,3,384,384]{4,3,2,1,0:T(8,128)(2,1)}, bf16[1,1,3,384,384]{4,3,2,1,0:T(8,128)(2,1)}, bf16[1,1,3,384,384]{4,3,2,1,0:T(8,128)(2,1)}, bf16[1,1...) fusion(bf16[3,3,3,384,384]{4,3,2,1,0:T(8,128)(2,1)} %param.12), kind=kLoop, calls=%fused_computation.94 | loop fusion | bytes 15925248 | tf_op jit(solution)/shard_map/slice | solution.py:74
  13.4 1.3 collective-permute-start.2
  14.7 5.5 %collective-permute-start.1 = (bf16[8,2,128,16]{2,3,1,0:T(8,128)(2,1)S(1)}, bf16[8,2,128,16]{2,3,1,0:T(8,128)(2,1)S(1)}, u32[]{:S(2)}, u32[]{:S(2)}) collective-permute-start(bf16[8,2,128,16]{2,3,1,0:T(8,128)(2,1)S(1)} %pad_maximum_fusion.11), channel_id=1, source_target_pairs={{0,2},{2,4},{4,6},{6,8},{8,10},{10,12},{12,14},{1,3},{3,5},{5,7},{... | collective-permute-start | bytes 196616 | tf_op jit(solution)/shard_map/ppermute | solution.py:25
  20.6 1.6 %collective-permute-done.1 = bf16[8,2,128,16]{2,3,1,0:T(8,128)(2,1)S(1)} collective-permute-done((bf16[8,2,128,16]{2,3,1,0:T(8,128)(2,1)S(1)}, bf16[8,2,128,16]{2,3,1,0:T(8,128)(2,1)S(1)}, u32[]{:S(2)}, u32[]{:S(2)}) %collective-permute-start.1) | collective-permute-done | bytes 65568 | tf_op jit(solution)/shard_map/ppermute | solution.py:25
  24.5 1.0 copy.18
  25.6 3.2 %reshape.112 = bf16[3072,432]{0,1:T(8,128)(2,1)} reshape(bf16[6,4,128,432]{2,1,0,3:T(4,128)(2,1)S(1)} %copy.18) | data formatting | bytes 5308416 | tf_op jit(solution)/shard_map/reshape | solution.py:49
  28.7 3.6 %add_convert_fusion = bf16[3072,384]{1,0:T(8,128)(2,1)S(1)} fusion(bf16[3072,432]{0,1:T(8,128)(2,1)} %reshape.112, bf16[432,384]{1,0:T(8,128)(2,1)S(1)} %bitcast.49, f32[384]{0:T(512)S(1)} %copy-done.14), kind=kOutput, calls=%fused_computation.1 | convolution fusion | flops 1021575168 | bytes 5346816 | tf_op jit(solution)/shard_map/dot_general | solution.py:50
  32.8 32.9 %psum.14 = f32[32]{0:T(128)S(1)} all-reduce(f32[32]{0:T(128)S(1)} %reduce_sum.25), channel_id=1, replica_groups=mesh['clip'=2,'ha'=8,'ta'=2] {'ha','ta'}, use_global_device_ids=true, to_apply=%region_2.3 | all-reduce | flops 32 | bytes 256 | tf_op jit(solution)/shard_map/psum | solution.py:109
  66.5 29.7 %psum.15 = f32[32]{0:T(128)S(1)} all-reduce(f32[32]{0:T(128)S(1)} %reduce_sum.37), channel_id=1, replica_groups=mesh['clip'=2,'ha'=8,'ta'=2] {'ha','ta'}, use_global_device_ids=true, to_apply=%region_5.6 | all-reduce | flops 32 | bytes 256 | tf_op jit(solution)/shard_map/psum | solution.py:111
  96.4 1.9 %fusion = bf16[6,4,128,384]{3,2,1,0:T(8,128)(2,1)S(1)} fusion(bf16[6,4,128,384]{3,2,1,0:T(8,128)(2,1)S(1)} %bitcast.53, f32[384]{0:T(512)S(1)} %copy-done.11, f32[384]{0:T(512)S(1)} %copy-done.12, f32[384]{0:T(512)S(1)} %mul.34, f32[384]{0:T(512)S(1)} %sub.26, pred[6,4]{1,0:T(8,128)(4,1)S(1)} %and_and_fusion), kind=kLoop, calls=%fused_computation.5 | loop fusion | flops 12976128 | bytes 4724760 | tf_op jit(solution)/shard_map/jit(_where)/select_n | solution.py:120
  98.3 3.6 %pad_slice_fusion.18 = (bf16[4,2,128,384]{3,2,1,0:T(8,128)(2,1)S(1)}, bf16[4,2,128,384]{3,2,1,0:T(8,128)(2,1)S(1)}, bf16[4,2,128,384]{3,2,1,0:T(8,128)(2,1)S(1)}...) fusion(bf16[6,4,128,384]{3,2,1,0:T(8,128)(2,1)S(1)} %fusion), kind=kLoop, calls=%fused_computation.76 | loop fusion | bytes 13369344 | tf_op jit(solution)/shard_map/slice | solution.py:63
  102.6 3.8 %pad_slice_fusion.19 = (bf16[4,2,128,384]{3,2,1,0:T(8,128)(2,1)S(1)}, bf16[4,2,128,384]{3,2,1,0:T(8,128)(2,1)S(1)}, bf16[4,2,128,384]{3,2,1,0:T(8,128)(2,1)S(1)}...) fusion(bf16[6,4,128,384]{3,2,1,0:T(8,128)(2,1)S(1)} %fusion), kind=kLoop, calls=%fused_computation.77 | loop fusion | bytes 11010048 | tf_op jit(solution)/shard_map/slice | solution.py:63
  107.6 1.4 %fusion.34 = f32[1024,384]{1,0:T(8,128)S(1)} fusion(bf16[1024,1152]{1,0:T(8,128)(2,1)S(1)} %bitcast.55, bf16[1152,384]{1,0:T(8,128)(2,1)S(1)} %bitcast.72), kind=kOutput, calls=%fused_computation.103 | convolution fusion | flops 905969664 | bytes 4816896 | tf_op jit(solution)/shard_map/dot_general | solution.py:72
  110.2 1.4 %fusion.33 = f32[1024,384]{1,0:T(8,128)S(1)} fusion(bf16[1024,1152]{1,0:T(8,128)(2,1)S(1)} %bitcast.56, bf16[1152,384]{1,0:T(8,128)(2,1)S(1)} %bitcast.71), kind=kOutput, calls=%fused_computation.102 | convolution fusion | flops 905969664 | bytes 4816896 | tf_op jit(solution)/shard_map/dot_general | solution.py:72
  112.8 1.4 %fusion.32 = f32[1024,384]{1,0:T(8,128)S(1)} fusion(bf16[1024,1152]{1,0:T(8,128)(2,1)S(1)} %bitcast.57, bf16[1152,384]{1,0:T(8,128)(2,1)S(1)} %bitcast.70), kind=kOutput, calls=%fused_computation.101 | convolution fusion | flops 905969664 | bytes 4816896 | tf_op jit(solution)/shard_map/dot_general | solution.py:72
  115.4 1.4 %fusion.31 = f32[1024,384]{1,0:T(8,128)S(1)} fusion(bf16[1024,1152]{1,0:T(8,128)(2,1)S(1)} %bitcast.58, bf16[1152,384]{1,0:T(8,128)(2,1)S(1)} %bitcast.69), kind=kOutput, calls=%fused_computation.100 | convolution fusion | flops 905969664 | bytes 4816896 | tf_op jit(solution)/shard_map/dot_general | solution.py:72
  118.0 1.4 %fusion.30 = f32[1024,384]{1,0:T(8,128)S(1)} fusion(bf16[1024,1152]{1,0:T(8,128)(2,1)S(1)} %bitcast.59, bf16[1152,384]{1,0:T(8,128)(2,1)S(1)} %bitcast.68), kind=kOutput, calls=%fused_computation.99 | convolution fusion | flops 905969664 | bytes 4816896 | tf_op jit(solution)/shard_map/dot_general | solution.py:72
  120.6 1.4 %fusion.29 = f32[1024,384]{1,0:T(8,128)S(1)} fusion(bf16[1024,1152]{1,0:T(8,128)(2,1)S(1)} %bitcast.60, bf16[1152,384]{1,0:T(8,128)(2,1)S(1)} %bitcast.67), kind=kOutput, calls=%fused_computation.98 | convolution fusion | flops 905969664 | bytes 4816896 | tf_op jit(solution)/shard_map/dot_general | solution.py:72
  123.2 1.4 %fusion.27 = f32[1024,384]{1,0:T(8,128)S(1)} fusion(bf16[1024,1152]{1,0:T(8,128)(2,1)S(1)} %bitcast.61, bf16[1152,384]{1,0:T(8,128)(2,1)S(1)} %bitcast.66), kind=kOutput, calls=%fused_computation.96 | convolution fusion | flops 905969664 | bytes 4816896 | tf_op jit(solution)/shard_map/dot_general | solution.py:72
  125.8 1.4 %fusion.28 = f32[1024,384]{1,0:T(8,128)S(1)} fusion(bf16[1024,1152]{1,0:T(8,128)(2,1)S(1)} %bitcast.62, bf16[1152,384]{1,0:T(8,128)(2,1)S(1)} %bitcast.65), kind=kOutput, calls=%fused_computation.97 | convolution fusion | flops 905969664 | bytes 4816896 | tf_op jit(solution)/shard_map/dot_general | solution.py:72
  128.5 1.7 %add_add_fusion = f32[1024,384]{1,0:T(8,128)S(1)} fusion(f32[1024,384]{1,0:T(8,128)S(1)} %fusion.34, f32[1024,384]{1,0:T(8,128)S(1)} %fusion.33, f32[1024,384]{1,0:T(8,128)S(1)} %fusion.32, f32[1024,384]{1,0:T(8,128)S(1)} %fusion.31, f32[1024,384]{1,0:T(8,128)S(1)} %fusion.30, f32[1024,384]{1,0:T(8,128)S(1)} %fusion.29, f32[1024,384]{1,0:T(8,128)S(1)} %fusion.27, ...), kind=kOutput, calls=%fused_computation.19 | convolution fusion | flops 909115392 | bytes 17399808 | tf_op jit(solution)/shard_map/dot_general | solution.py:72
  130.2 1.1 fusion.4
  (95 shorter events, 16.7 us)
Async XLA Ops:
  0.0 28.7 %copy-start = (bf16[3,3,3,16,384]{4,3,2,1,0:T(8,128)(2,1)S(1)}, bf16[3,3,3,16,384]{4,3,2,1,0:T(8,128)(2,1)}, u32[]{:S(2)}) copy-start(bf16[3,3,3,16,384]{4,3,2,1,0:T(8,128)(2,1)} %param.8) | copy-start | bytes 995332
  5.3 8.0 %collective-permute-start = (bf16[4,2,128,16]{3,2,1,0:T(8,128)(2,1)S(1)}, bf16[4,2,128,16]{3,2,1,0:T(8,128)(2,1)S(1)}, u32[]{:S(2)}, u32[]{:S(2)}) collective-permute-start(bf16[4,2,128,16]{3,2,1,0:T(8,128)(2,1)S(1)} %bitcast.63), channel_id=1, source_target_pairs={{0,1},{2,3},{4,5},{6,7},{8,9},{10,11},{12,13},{14,15},{16,17},{18,... | collective-permute-start | bytes 98312 | tf_op jit(solution)/shard_map/ppermute | solution.py:15
  13.4 7.1 %collective-permute-start.2 = (bf16[8,2,128,16]{2,3,1,0:T(8,128)(2,1)S(1)}, bf16[8,2,128,16]{2,3,1,0:T(8,128)(2,1)S(1)}, u32[]{:S(2)}, u32[]{:S(2)}) collective-permute-start(bf16[8,2,128,16]{2,3,1,0:T(8,128)(2,1)S(1)} %pad_maximum_fusion.11), channel_id=1, source_target_pairs={{2,0},{4,2},{6,4},{8,6},{10,8},{12,10},{14,12},{3,1},{5,3},{7,5},{... | collective-permute-start | bytes 196616 | tf_op jit(solution)/shard_map/ppermute | solution.py:26
  14.7 7.4 %collective-permute-start.1 = (bf16[8,2,128,16]{2,3,1,0:T(8,128)(2,1)S(1)}, bf16[8,2,128,16]{2,3,1,0:T(8,128)(2,1)S(1)}, u32[]{:S(2)}, u32[]{:S(2)}) collective-permute-start(bf16[8,2,128,16]{2,3,1,0:T(8,128)(2,1)S(1)} %pad_maximum_fusion.11), channel_id=1, source_target_pairs={{0,2},{2,4},{4,6},{6,8},{8,10},{10,12},{12,14},{1,3},{3,5},{5,7},{... | collective-permute-start | bytes 196616 | tf_op jit(solution)/shard_map/ppermute | solution.py:25
  25.5 3.2 %copy-start.14 = (f32[384]{0:T(512)S(1)}, f32[384]{0:T(512)}, u32[]{:S(2)}) copy-start(f32[384]{0:T(512)} %param.9) | copy-start | bytes 4612
  32.3 64.0 %copy-start.11 = (f32[384]{0:T(512)S(1)}, f32[384]{0:T(512)}, u32[]{:S(2)}) copy-start(f32[384]{0:T(512)} %param.11) | copy-start | bytes 4612
  32.3 64.0 %copy-start.12 = (f32[384]{0:T(512)S(1)}, f32[384]{0:T(512)}, u32[]{:S(2)}) copy-start(f32[384]{0:T(512)} %param.10) | copy-start | bytes 4612
  106.4 1.2 copy-start.10
  109.0 1.2 copy-start.9
  111.6 1.2 copy-start.8
  114.2 1.2 copy-start.7
  116.8 1.2 copy-start.6
  119.5 1.2 copy-start.5
  122.1 1.2 copy-start.4
  124.7 1.2 copy-start.3
  127.3 1.2 copy-start.2
  128.5 1.8 %copy-start.13 = (f32[384]{0:T(512)S(1)}, f32[384]{0:T(512)}, u32[]{:S(2)}) copy-start(f32[384]{0:T(512)} %param.13) | copy-start | bytes 4612
  128.5 2.9 %copy-start.1 = (bf16[3,3,3,16,384]{4,3,2,1,0:T(8,128)(2,1)S(1)}, bf16[3,3,3,16,384]{4,3,2,1,0:T(8,128)(2,1)}, u32[]{:S(2)}) copy-start(bf16[3,3,3,16,384]{4,3,2,1,0:T(8,128)(2,1)} %param.8) | copy-start | bytes 995332
where the time goes:
time: 132 us; the launch traced here: 131 us
  blocking collectives  66.4 us (50%)
  local copies, waits for them, and re-layouts  30.3 us (23%)
  matrix products  16.8 us (13%)
  starting transfers between devices  8.88 us (7%)
  other arithmetic  6.55 us (5%)
  waiting for transfers between devices  1.81 us (1%)
    psum x1, blocking collectives, body(): mean = lax.psum(group_totals(values), ('ha', 'ta')) / count  32.9 us
    psum x1, blocking collectives, body(): var = lax.psum(group_totals(centered * centered), ('ha', 'ta')) / count  29.7 us
    dot_general x9, matrix products, middle_conv(): jnp.dot(slab, w_mid[frame_tap, row_tap].reshape(3 * channels, -1), prefer...  13.2 us
    unnamed x58, local copies, waits for them, and re-layouts  10.8 us
    slice x3, local copies, waits for them, and re-layouts, middle_conv(): padded[frame_tap:frame_tap + frames, row_tap:row_tap + rows, col_tap:col_...  8.12 us
    slice x1, local copies, waits for them, and re-layouts, middle_conv(): w_mid[frame_tap, row_tap].reshape(3 * channels, -1)  5.75 us
    ppermute x1, starting transfers between devices, extended_2(): before = lax.ppermute(last, axis, up)  5.5 us
    all_to_all x1, blocking collectives, body(): lax.all_to_all(latent_tokens, 'ta', split_axis=0, concat_axis=1, tiled=True)  3.75 us
  transfers between devices with their start and end apart: 3, of which 2 were waited for; matrix products, arithmetic and copies ran while one was open for 5% of the time, Pallas kernels for 0%

commit v1 on v0

--- a/solution.py
+++ b/solution.py
@@ -7,6 +7,11 @@
 H_DEV = 2
 W = 128
 eps = 1e-06
+
+
+def one_after_other(value_2, inner_axis, outer_axis):
+    half = lax.psum(value_2, inner_axis)
+    return lax.psum(half, outer_axis)
 
 
 def passed_along(value, axis, by):
@@ -106,7 +111,7 @@
     values = lax.optimization_barrier(hidden).astype(jnp.float32)
     members = values.shape[-1] // GROUPS
     count = float(lax.axis_size("ha") * lax.axis_size("ta") * frames * rows * cols * members)
-    mean = lax.psum(group_totals(values), ("ha", "ta")) / count
+    mean = one_after_other(group_totals(values), "ta", "ha") / count
     centered = values - jnp.repeat(mean, members)
     var = lax.psum(group_totals(centered * centered), ("ha", "ta")) / count
     active = normalize(wide_hidden, mean, var, gn_gain, gn_shift)

time: 132 us -> 125 us (0.947)
  blocking collectives: 66.4 us -> 58.9 us
    psum x1 -> x2, blocking collectives: 32.9 us -> 25.5 us  [the longest x1 23 us: one_after_other(): return lax.psum(half, outer_axis)]
where the time goes in v1:
time: 125 us; the launch traced here: 124 us
  blocking collectives  58.9 us (47%)
  local copies, waits for them, and re-layouts  30.3 us (24%)
  matrix products  16.8 us (13%)
  starting transfers between devices  8.88 us (7%)
  other arithmetic  6.55 us (5%)
  waiting for transfers between devices  1.81 us (1%)
    psum x1, blocking collectives, body(): var = lax.psum(group_totals(centered * centered), ('ha', 'ta')) / count  29.7 us
    psum x1, blocking collectives, one_after_other(): return lax.psum(half, outer_axis)  23 us
    dot_general x9, matrix products, middle_conv(): jnp.dot(slab, w_mid[frame_tap, row_tap].reshape(3 * channels, -1), prefer...  13.2 us
    unnamed x58, local copies, waits for them, and re-layouts  10.8 us
    slice x3, local copies, waits for them, and re-layouts, middle_conv(): padded[frame_tap:frame_tap + frames, row_tap:row_tap + rows, col_tap:col_...  8.12 us
    slice x1, local copies, waits for them, and re-layouts, middle_conv(): w_mid[frame_tap, row_tap].reshape(3 * channels, -1)  5.74 us
    ppermute x1, starting transfers between devices, extended_2(): before = lax.ppermute(last, axis, up)  5.5 us
    all_to_all x1, blocking collectives, body(): lax.all_to_all(latent_tokens, 'ta', split_axis=0, concat_axis=1, tiled=True)  3.75 us
  transfers between devices with their start and end apart: 3, of which 2 were waited for; matrix products, arithmetic and copies ran while one was open for 5% of the time, Pallas kernels for 0%

profile of v1, /device:TPU:0, one launch (start us, length us, event | category | flops | bytes accessed | tf_op | source)
XLA Modules:
  0.0 123.9 jit_solution(14839199736923180877)
XLA Ops:
  1.0 3.7 %all_to_all.15 = bf16[2,2,4096]{2,1,0:T(2,128)(2,1)S(1)} all-to-all(bf16[2,2,4096]{2,1,0:T(2,128)(2,1)S(1)} %reshape.124), channel_id=1, replica_groups=mesh['clip'=2,'ha'=8,'ta'=2] {'ta'}, dimensions={0} | all-to-all | bytes 65536 | tf_op jit(solution)/shard_map/all_to_all | solution.py:101
  5.3 2.1 %collective-permute-start = (bf16[4,2,128,16]{3,2,1,0:T(8,128)(2,1)S(1)}, bf16[4,2,128,16]{3,2,1,0:T(8,128)(2,1)S(1)}, u32[]{:S(2)}, u32[]{:S(2)}) collective-permute-start(bf16[4,2,128,16]{3,2,1,0:T(8,128)(2,1)S(1)} %bitcast.63), channel_id=1, source_target_pairs={{0,1},{2,3},{4,5},{6,7},{8,9},{10,11},{12,13},{14,15},{16,17},{18,... | collective-permute-start | bytes 98312 | tf_op jit(solution)/shard_map/ppermute | solution.py:20
  7.4 5.7 %fusion.25 = (bf16[1,1,3,384,384]{4,3,2,1,0:T(8,128)(2,1)}, bf16[1,1,3,384,384]{4,3,2,1,0:T(8,128)(2,1)}, bf16[1,1,3,384,384]{4,3,2,1,0:T(8,128)(2,1)}, bf16[1,1...) fusion(bf16[3,3,3,384,384]{4,3,2,1,0:T(8,128)(2,1)} %param.12), kind=kLoop, calls=%fused_computation.94 | loop fusion | bytes 15925248 | tf_op jit(solution)/shard_map/slice | solution.py:79
  13.4 1.3 %collective-permute-start.2 = (bf16[8,2,128,16]{2,3,1,0:T(8,128)(2,1)S(1)}, bf16[8,2,128,16]{2,3,1,0:T(8,128)(2,1)S(1)}, u32[]{:S(2)}, u32[]{:S(2)}) collective-permute-start(bf16[8,2,128,16]{2,3,1,0:T(8,128)(2,1)S(1)} %pad_maximum_fusion.11), channel_id=1, source_target_pairs={{2,0},{4,2},{6,4},{8,6},{10,8},{12,10},{14,12},{3,1},{5,3},{7,5},{... | collective-permute-start | bytes 196616 | tf_op jit(solution)/shard_map/ppermute | solution.py:31
  14.7 5.5 %collective-permute-start.1 = (bf16[8,2,128,16]{2,3,1,0:T(8,128)(2,1)S(1)}, bf16[8,2,128,16]{2,3,1,0:T(8,128)(2,1)S(1)}, u32[]{:S(2)}, u32[]{:S(2)}) collective-permute-start(bf16[8,2,128,16]{2,3,1,0:T(8,128)(2,1)S(1)} %pad_maximum_fusion.11), channel_id=1, source_target_pairs={{0,2},{2,4},{4,6},{6,8},{8,10},{10,12},{12,14},{1,3},{3,5},{5,7},{... | collective-permute-start | bytes 196616 | tf_op jit(solution)/shard_map/ppermute | solution.py:30
  20.6 1.6 %collective-permute-done.1 = bf16[8,2,128,16]{2,3,1,0:T(8,128)(2,1)S(1)} collective-permute-done((bf16[8,2,128,16]{2,3,1,0:T(8,128)(2,1)S(1)}, bf16[8,2,128,16]{2,3,1,0:T(8,128)(2,1)S(1)}, u32[]{:S(2)}, u32[]{:S(2)}) %collective-permute-start.1) | collective-permute-done | bytes 65568 | tf_op jit(solution)/shard_map/ppermute | solution.py:30
  25.5 3.1 %reshape.112 = bf16[3072,432]{0,1:T(8,128)(2,1)} reshape(bf16[6,4,128,432]{2,1,0,3:T(4,128)(2,1)S(1)} %copy.18) | data formatting | bytes 5308416 | tf_op jit(solution)/shard_map/reshape | solution.py:54
  28.7 3.6 %add_convert_fusion = bf16[3072,384]{1,0:T(8,128)(2,1)S(1)} fusion(bf16[3072,432]{0,1:T(8,128)(2,1)} %reshape.112, bf16[432,384]{1,0:T(8,128)(2,1)S(1)} %bitcast.49, f32[384]{0:T(512)S(1)} %copy-done.14), kind=kOutput, calls=%fused_computation.1 | convolution fusion | flops 1021575168 | bytes 5346816 | tf_op jit(solution)/shard_map/dot_general | solution.py:55
  32.8 2.5 %psum.21 = f32[32]{0:T(128)S(1)} all-reduce(f32[32]{0:T(128)S(1)} %reduce_sum.25), channel_id=1, replica_groups=mesh['clip'=2,'ha'=8,'ta'=2] {'ta'}, use_global_device_ids=true, to_apply=%region_2.3 | all-reduce | flops 32 | bytes 256 | tf_op jit(solution)/shard_map/psum | solution.py:13
  35.3 23.0 %psum.22 = f32[32]{0:T(128)S(1)} all-reduce(f32[32]{0:T(128)S(1)} %psum.21), channel_id=1, replica_groups=mesh['clip'=2,'ha'=8,'ta'=2] {'ha'}, use_global_device_ids=true, to_apply=%region_3.4 | all-reduce | flops 32 | bytes 256 | tf_op jit(solution)/shard_map/psum | solution.py:14
  59.0 29.7 %psum.23 = f32[32]{0:T(128)S(1)} all-reduce(f32[32]{0:T(128)S(1)} %reduce_sum.37), channel_id=1, replica_groups=mesh['clip'=2,'ha'=8,'ta'=2] {'ha','ta'}, use_global_device_ids=true, to_apply=%region_6.7 | all-reduce | flops 32 | bytes 256 | tf_op jit(solution)/shard_map/psum | solution.py:116
  88.9 1.9 %fusion = bf16[6,4,128,384]{3,2,1,0:T(8,128)(2,1)S(1)} fusion(bf16[6,4,128,384]{3,2,1,0:T(8,128)(2,1)S(1)} %bitcast.53, f32[384]{0:T(512)S(1)} %copy-done.11, f32[384]{0:T(512)S(1)} %copy-done.12, f32[384]{0:T(512)S(1)} %mul.34, f32[384]{0:T(512)S(1)} %sub.26, pred[6,4]{1,0:T(8,128)(4,1)S(1)} %and_and_fusion), kind=kLoop, calls=%fused_computation.5 | loop fusion | flops 12976128 | bytes 4724760 | tf_op jit(solution)/shard_map/jit(_where)/select_n | solution.py:125
  90.8 3.6 %pad_slice_fusion.18 = (bf16[4,2,128,384]{3,2,1,0:T(8,128)(2,1)S(1)}, bf16[4,2,128,384]{3,2,1,0:T(8,128)(2,1)S(1)}, bf16[4,2,128,384]{3,2,1,0:T(8,128)(2,1)S(1)}...) fusion(bf16[6,4,128,384]{3,2,1,0:T(8,128)(2,1)S(1)} %fusion), kind=kLoop, calls=%fused_computation.76 | loop fusion | bytes 13369344 | tf_op jit(solution)/shard_map/slice | solution.py:68
  95.1 3.8 %pad_slice_fusion.19 = (bf16[4,2,128,384]{3,2,1,0:T(8,128)(2,1)S(1)}, bf16[4,2,128,384]{3,2,1,0:T(8,128)(2,1)S(1)}, bf16[4,2,128,384]{3,2,1,0:T(8,128)(2,1)S(1)}...) fusion(bf16[6,4,128,384]{3,2,1,0:T(8,128)(2,1)S(1)} %fusion), kind=kLoop, calls=%fused_computation.77 | loop fusion | bytes 11010048 | tf_op jit(solution)/shard_map/slice | solution.py:68
  100.1 1.4 %fusion.34 = f32[1024,384]{1,0:T(8,128)S(1)} fusion(bf16[1024,1152]{1,0:T(8,128)(2,1)S(1)} %bitcast.55, bf16[1152,384]{1,0:T(8,128)(2,1)S(1)} %bitcast.72), kind=kOutput, calls=%fused_computation.103 | convolution fusion | flops 905969664 | bytes 4816896 | tf_op jit(solution)/shard_map/dot_general | solution.py:77
  102.7 1.4 %fusion.33 = f32[1024,384]{1,0:T(8,128)S(1)} fusion(bf16[1024,1152]{1,0:T(8,128)(2,1)S(1)} %bitcast.56, bf16[1152,384]{1,0:T(8,128)(2,1)S(1)} %bitcast.71), kind=kOutput, calls=%fused_computation.102 | convolution fusion | flops 905969664 | bytes 4816896 | tf_op jit(solution)/shard_map/dot_general | solution.py:77
  105.3 1.4 %fusion.32 = f32[1024,384]{1,0:T(8,128)S(1)} fusion(bf16[1024,1152]{1,0:T(8,128)(2,1)S(1)} %bitcast.57, bf16[1152,384]{1,0:T(8,128)(2,1)S(1)} %bitcast.70), kind=kOutput, calls=%fused_computation.101 | convolution fusion | flops 905969664 | bytes 4816896 | tf_op jit(solution)/shard_map/dot_general | solution.py:77
  107.9 1.4 %fusion.31 = f32[1024,384]{1,0:T(8,128)S(1)} fusion(bf16[1024,1152]{1,0:T(8,128)(2,1)S(1)} %bitcast.58, bf16[1152,384]{1,0:T(8,128)(2,1)S(1)} %bitcast.69), kind=kOutput, calls=%fused_computation.100 | convolution fusion | flops 905969664 | bytes 4816896 | tf_op jit(solution)/shard_map/dot_general | solution.py:77
  110.5 1.4 %fusion.30 = f32[1024,384]{1,0:T(8,128)S(1)} fusion(bf16[1024,1152]{1,0:T(8,128)(2,1)S(1)} %bitcast.59, bf16[1152,384]{1,0:T(8,128)(2,1)S(1)} %bitcast.68), kind=kOutput, calls=%fused_computation.99 | convolution fusion | flops 905969664 | bytes 4816896 | tf_op jit(solution)/shard_map/dot_general | solution.py:77
  113.2 1.4 %fusion.29 = f32[1024,384]{1,0:T(8,128)S(1)} fusion(bf16[1024,1152]{1,0:T(8,128)(2,1)S(1)} %bitcast.60, bf16[1152,384]{1,0:T(8,128)(2,1)S(1)} %bitcast.67), kind=kOutput, calls=%fused_computation.98 | convolution fusion | flops 905969664 | bytes 4816896 | tf_op jit(solution)/shard_map/dot_general | solution.py:77
  115.8 1.4 %fusion.27 = f32[1024,384]{1,0:T(8,128)S(1)} fusion(bf16[1024,1152]{1,0:T(8,128)(2,1)S(1)} %bitcast.61, bf16[1152,384]{1,0:T(8,128)(2,1)S(1)} %bitcast.66), kind=kOutput, calls=%fused_computation.96 | convolution fusion | flops 905969664 | bytes 4816896 | tf_op jit(solution)/shard_map/dot_general | solution.py:77
  118.4 1.4 %fusion.28 = f32[1024,384]{1,0:T(8,128)S(1)} fusion(bf16[1024,1152]{1,0:T(8,128)(2,1)S(1)} %bitcast.62, bf16[1152,384]{1,0:T(8,128)(2,1)S(1)} %bitcast.65), kind=kOutput, calls=%fused_computation.97 | convolution fusion | flops 905969664 | bytes 4816896 | tf_op jit(solution)/shard_map/dot_general | solution.py:77
  121.0 1.7 %add_add_fusion = f32[1024,384]{1,0:T(8,128)S(1)} fusion(f32[1024,384]{1,0:T(8,128)S(1)} %fusion.34, f32[1024,384]{1,0:T(8,128)S(1)} %fusion.33, f32[1024,384]{1,0:T(8,128)S(1)} %fusion.32, f32[1024,384]{1,0:T(8,128)S(1)} %fusion.31, f32[1024,384]{1,0:T(8,128)S(1)} %fusion.30, f32[1024,384]{1,0:T(8,128)S(1)} %fusion.29, f32[1024,384]{1,0:T(8,128)S(1)} %fusion.27, ...), kind=kOutput, calls=%fused_computation.19 | convolution fusion | flops 909115392 | bytes 17399808 | tf_op jit(solution)/shard_map/dot_general | solution.py:77
  122.7 1.1 fusion.4
  (96 shorter events, 17.7 us)
Async XLA Ops:
  0.0 28.7 %copy-start = (bf16[3,3,3,16,384]{4,3,2,1,0:T(8,128)(2,1)S(1)}, bf16[3,3,3,16,384]{4,3,2,1,0:T(8,128)(2,1)}, u32[]{:S(2)}) copy-start(bf16[3,3,3,16,384]{4,3,2,1,0:T(8,128)(2,1)} %param.8) | copy-start | bytes 995332
  5.3 8.0 %collective-permute-start = (bf16[4,2,128,16]{3,2,1,0:T(8,128)(2,1)S(1)}, bf16[4,2,128,16]{3,2,1,0:T(8,128)(2,1)S(1)}, u32[]{:S(2)}, u32[]{:S(2)}) collective-permute-start(bf16[4,2,128,16]{3,2,1,0:T(8,128)(2,1)S(1)} %bitcast.63), channel_id=1, source_target_pairs={{0,1},{2,3},{4,5},{6,7},{8,9},{10,11},{12,13},{14,15},{16,17},{18,... | collective-permute-start | bytes 98312 | tf_op jit(solution)/shard_map/ppermute | solution.py:20
  13.4 7.1 %collective-permute-start.2 = (bf16[8,2,128,16]{2,3,1,0:T(8,128)(2,1)S(1)}, bf16[8,2,128,16]{2,3,1,0:T(8,128)(2,1)S(1)}, u32[]{:S(2)}, u32[]{:S(2)}) collective-permute-start(bf16[8,2,128,16]{2,3,1,0:T(8,128)(2,1)S(1)} %pad_maximum_fusion.11), channel_id=1, source_target_pairs={{2,0},{4,2},{6,4},{8,6},{10,8},{12,10},{14,12},{3,1},{5,3},{7,5},{... | collective-permute-start | bytes 196616 | tf_op jit(solution)/shard_map/ppermute | solution.py:31
  14.7 7.4 %collective-permute-start.1 = (bf16[8,2,128,16]{2,3,1,0:T(8,128)(2,1)S(1)}, bf16[8,2,128,16]{2,3,1,0:T(8,128)(2,1)S(1)}, u32[]{:S(2)}, u32[]{:S(2)}) collective-permute-start(bf16[8,2,128,16]{2,3,1,0:T(8,128)(2,1)S(1)} %pad_maximum_fusion.11), channel_id=1, source_target_pairs={{0,2},{2,4},{4,6},{6,8},{8,10},{10,12},{12,14},{1,3},{3,5},{5,7},{... | collective-permute-start | bytes 196616 | tf_op jit(solution)/shard_map/ppermute | solution.py:30
  25.5 3.2 %copy-start.14 = (f32[384]{0:T(512)S(1)}, f32[384]{0:T(512)}, u32[]{:S(2)}) copy-start(f32[384]{0:T(512)} %param.9) | copy-start | bytes 4612
  32.3 56.6 %copy-start.11 = (f32[384]{0:T(512)S(1)}, f32[384]{0:T(512)}, u32[]{:S(2)}) copy-start(f32[384]{0:T(512)} %param.11) | copy-start | bytes 4612
  32.3 56.6 %copy-start.12 = (f32[384]{0:T(512)S(1)}, f32[384]{0:T(512)}, u32[]{:S(2)}) copy-start(f32[384]{0:T(512)} %param.10) | copy-start | bytes 4612
  98.9 1.2 copy-start.10
  101.5 1.2 copy-start.9
  104.2 1.2 copy-start.8
  106.8 1.2 copy-start.7
  109.4 1.2 copy-start.6
  112.0 1.2 copy-start.5
  114.6 1.2 copy-start.4
  117.2 1.2 copy-start.3
  119.8 1.2 copy-start.2
  121.0 1.8 %copy-start.13 = (f32[384]{0:T(512)S(1)}, f32[384]{0:T(512)}, u32[]{:S(2)}) copy-start(f32[384]{0:T(512)} %param.13) | copy-start | bytes 4612
  121.0 2.9 %copy-start.1 = (bf16[3,3,3,16,384]{4,3,2,1,0:T(8,128)(2,1)S(1)}, bf16[3,3,3,16,384]{4,3,2,1,0:T(8,128)(2,1)}, u32[]{:S(2)}) copy-start(bf16[3,3,3,16,384]{4,3,2,1,0:T(8,128)(2,1)} %param.8) | copy-start | bytes 995332
